TPU v7x, 32 devices: a whole 2x2x4 slice. The times are simulated.
32 devices in a mesh: rep: 4 (over z), row: 4 (over x, core), col: 2 (over y).
Axes of the slice: x: 2, y: 2, z: 4, core: 2. Of those that a mesh axis runs over, the one named last changes fastest.
Arguments:
- grad_parts: bfloat16 [4, 16384, 6144], P('rep', ('row', 'col')), may hold values from -0.03125 to 0.03125, as said below
- statistic: float32 [6144, 6144], P('row', 'col'), may hold values from -150 to 150, as said below
Outputs:
- gram_matrix: float32 [6144, 6144], P('row', 'col')
- statistic_next: float32 [6144, 6144], P('row', 'col')
Inputs may be any that keep to these rules, and one draw needn't show every extreme that they name: Every entry of grad_parts has a magnitude between 2^-10 and 2^-5. statistic is symmetric and positive definite.
All inputs are finite; a program needn't handle non-finite values.
Results may differ from a plain program's by a relative error of at most 0.008.
Values may be sent and summed in bfloat16 or wider, within the bound.
A program may use at most 192 MiB of HBM per device.

v0:
```python
import jax
import jax.numpy as jnp
from jax import lax
from jax.sharding import PartitionSpec as P


def shards(grad_parts, statistic):
    own_part = grad_parts[0].astype(jnp.float32)
    summed = lax.psum_scatter(own_part.astype(jnp.bfloat16), "rep", scatter_dimension=0, tiled=True)
    rows_panel = lax.all_to_all(summed, "row", split_axis=1, concat_axis=0, tiled=True)
    cols_panel = lax.all_to_all(summed, "col", split_axis=1, concat_axis=0, tiled=True)
    row_count = lax.axis_size("row")
    col_count = lax.axis_size("col")
    quarter = summed.shape[0]
    left_whole = lax.all_gather(rows_panel, "col", axis=0, tiled=True)
    left_order = (
        left_whole.reshape(col_count, row_count, quarter, -1)
        .transpose(1, 0, 2, 3)
        .reshape(row_count * col_count * quarter, -1)
    )
    partial_tile = lax.dot_general(
        left_order,
        lax.all_gather(cols_panel, "row", axis=0, tiled=True),
        (((0,), (0,)), ((), ())),
        preferred_element_type=jnp.float32,
    )
    gram_tile = lax.psum(partial_tile, "rep")
    return (gram_tile, 0.95 * statistic + 0.05 * gram_tile)


def solution(mesh):
    return jax.shard_map(
        shards,
        mesh=mesh,
        in_specs=(P("rep", ("row", "col"), None), P("row", "col")),
        out_specs=(P("row", "col"), P("row", "col")),
        check_vma=False,
    )
```

profile of v0, /device:TPU:0, one launch (start us, length us, event | category | flops | bytes accessed | tf_op | source)
XLA Modules:
  0.0 1626.5 jit_solution(12246390620208611394)
XLA Ops:
  7.2 0.0 reduce-scatter.2.cloned.1.call-start
  7.2 30.3 %copy.5 = bf16[1,2048,6144]{1,2,0:T(8,128)(2,1)} copy(bf16[1,2048,6144]{2,1,0:T(8,128)(2,1)} %param.2) | data formatting | bytes 50331648 | tf_op args[0]
  37.5 0.0 reduce-scatter.2.cloned.1.call-update
  37.6 0.0 all-gather.3.cloned.1.call-start
  37.6 417.0 %reduce-scatter.2.cloned.1.call-done = bf16[512,6144]{0,1:T(8,128)(2,1)} async-done(((bf16[2048,6144]{0,1:T(8,128)(2,1)}), bf16[512,6144]{0,1:T(8,128)(2,1)}) %reduce-scatter.2.cloned.1.call-update) | async-done | bytes 6291472 | tf_op jit(solution)/shard_map/reduce_scatter | solution.py:9
  454.7 77.3 %all_to_all.38 = bf16[512,4,1536]{0,2,1:T(8,128)(2,1)} all-to-all(bf16[512,4,1536]{0,2,1:T(8,128)(2,1)} %bitcast.15), channel_id=1, replica_groups=mesh['rep'=4,'row'=4,'col'=2] {'row'}, dimensions={1} | all-to-all | bytes 12582912 | tf_op jit(solution)/shard_map/all_to_all | solution.py:10
  532.0 8.6 copy.6
  540.6 0.0 all-gather.3.cloned.1.call-update
  540.6 0.0 all-gather.5.cloned.1.call-start
  540.7 140.8 %all_to_all.39 = bf16[512,2,3072]{0,2,1:T(8,128)(2,1)} all-to-all(bf16[512,2,3072]{0,2,1:T(8,128)(2,1)} %bitcast.16), channel_id=1, replica_groups=mesh['rep'=4,'row'=4,'col'=2] {'col'}, dimensions={1} | all-to-all | bytes 12582912 | tf_op jit(solution)/shard_map/all_to_all | solution.py:11
  681.4 8.6 copy.8
  690.1 0.0 all-gather.5.cloned.1.call-update
  690.1 0.0 all-reduce.2.cloned.1.call-start
  690.2 64.5 %all-gather.3.cloned.1.call-done = bf16[4096,1536]{1,0:T(8,128)(2,1)} async-done(((bf16[2048,1536]{1,0:T(8,128)(2,1)}), bf16[4096,1536]{1,0:T(8,128)(2,1)}) %all-gather.3.cloned.1.call-update) | async-done | bytes 12582928 | tf_op jit(solution)/shard_map/all_gather | solution.py:15
  754.7 11.1 copy.7
  765.8 145.7 %all-gather.5.cloned.1.call-done = bf16[4096,3072]{1,0:T(8,128)(2,1)} async-done(((bf16[1024,3072]{1,0:T(8,128)(2,1)}), bf16[4096,3072]{1,0:T(8,128)(2,1)}) %all-gather.5.cloned.1.call-update) | async-done | bytes 25165840 | tf_op jit(solution)/shard_map/all_gather | solution.py:23
  911.5 48.0 %fusion = f32[1536,3072]{1,0:T(8,128)} fusion(bf16[4096,1536]{1,0:T(8,128)(2,1)} %bitcast.21, bf16[4096,3072]{1,0:T(8,128)(2,1)} %all-gather.5.cloned.1.call-done), kind=kOutput, calls=%fused_computation.1 | convolution fusion | flops 38654705664 | bytes 56623104 | tf_op jit(solution)/shard_map/dot_general | solution.py:21
  959.5 0.0 all-reduce.2.cloned.1.call-update
  959.6 629.5 %all-reduce.2.cloned.1.call-done = f32[1536,3072]{1,0:T(8,128)} async-done(((f32[1536,3072]{1,0:T(8,128)}), f32[1536,3072]{1,0:T(8,128)}) %all-reduce.2.cloned.1.call-update) | async-done | bytes 18874384 | tf_op jit(solution)/shard_map/psum | solution.py:27
  1589.1 0.0 copy-start
  1589.1 20.7 %multiply_add_fusion = f32[1536,3072]{1,0:T(8,128)} fusion(f32[1536,3072]{1,0:T(8,128)} %all-reduce.2.cloned.1.call-done, f32[1536,3072]{1,0:T(8,128)} %param.3), kind=kLoop, calls=%fused_computation | loop fusion | flops 14155776 | bytes 56623104 | tf_op jit(solution)/shard_map/add | solution.py:28
  1609.8 3.3 copy-done
  1613.1 6.8 copy.10
Async XLA Ops:
  7.2 447.5 %reduce-scatter.2.cloned.1.call-start = ((), (), s32[]{:S(2)}) async-start(), calls=%async_computation.3 | async-start | bytes 31457280 | tf_op jit(solution)/shard_map/reduce_scatter | solution.py:9
  37.6 717.1 %all-gather.3.cloned.1.call-start = ((), (), s32[]{:S(2)}) async-start(), calls=%async_computation.4 | async-start | bytes 18874368 | tf_op jit(solution)/shard_map/all_gather | solution.py:15
  540.6 370.9 %all-gather.5.cloned.1.call-start = ((), (), s32[]{:S(2)}) async-start(), calls=%async_computation.5 | async-start | bytes 31457280 | tf_op jit(solution)/shard_map/all_gather | solution.py:23
  690.1 899.0 %all-reduce.2.cloned.1.call-start = ((), (), s32[]{:S(2)}) async-start(), calls=%async_computation.6 | async-start | bytes 37748736 | tf_op jit(solution)/shard_map/psum | solution.py:27
  1589.1 24.0 %copy-start = (f32[1536,3072]{1,0:T(8,128)S(1)}, f32[1536,3072]{1,0:T(8,128)}, u32[]{:S(2)}) copy-start(f32[1536,3072]{1,0:T(8,128)} %all-reduce.2.cloned.1.call-done) | copy-start | bytes 56623108
Sparse Core Ops, SparseCore 0:
  37.7 416.9 reduce-scatter.1
  540.7 213.8 all-gather.2
  756.2 155.2 all-gather.4
  959.7 629.3 all-reduce.1
where the time goes:
time: 1630 us
  waiting for transfers between devices  1260 us (77%)
  blocking collectives  218 us (13%)
  local copies, waits for them, and re-layouts  68.9 us (4%)
  matrix products  48 us (3%)
  other arithmetic  20.7 us (1%)
    psum x1, waiting for transfers between devices, shards(): gram_tile = lax.psum(partial_tile, 'rep')  630 us
    reduce_scatter x1, waiting for transfers between devices, shards(): lax.psum_scatter(own_part.astype(jnp.bfloat16), 'rep', scatter_dimension=...  417 us
    all_gather x1, waiting for transfers between devices, shards(): lax.all_gather(cols_panel, 'row', axis=0, tiled=True)  146 us
    all_to_all x1, blocking collectives, shards(): lax.all_to_all(summed, 'col', split_axis=1, concat_axis=0, tiled=True)  141 us
    all_to_all x1, blocking collectives, shards(): lax.all_to_all(summed, 'row', split_axis=1, concat_axis=0, tiled=True)  77.3 us
    all_gather x1, waiting for transfers between devices, shards(): left_whole = lax.all_gather(rows_panel, 'col', axis=0, tiled=True)  64.5 us
    dot_general x1, matrix products, shards(): lax.dot_general(left_order, lax.all_gather(cols_panel, 'row', axis=0, til...  48 us
    unnamed x4, local copies, waits for them, and re-layouts  40.5 us
  transfers between devices with their start and end apart: 4, of which 4 were waited for; matrix products, arithmetic and copies ran while one was open for 1% of the time, Pallas kernels for 0%

commit v1 on v0

--- a/solution.py
+++ b/solution.py
@@ -24,7 +24,7 @@
         (((0,), (0,)), ((), ())),
         preferred_element_type=jnp.float32,
     )
-    gram_tile = lax.psum(partial_tile, "rep")
+    gram_tile = jnp.sum(lax.all_gather(partial_tile, "rep"), axis=0)
     return (gram_tile, 0.95 * statistic + 0.05 * gram_tile)
 
 

time: 1630 us -> 2270 us (1.39)
  waiting for transfers between devices: 1260 us -> 1880 us
  other arithmetic: 20.7 us -> 52 us
    all_gather x0 -> x1, waiting for transfers between devices: none -> 1250 us  [shards(): gram_tile = jnp.sum(lax.all_gather(partial_tile, 'rep'), axis=0)]
    psum x1 -> x0, waiting for transfers between devices: 630 us -> none  [shards(): gram_tile = lax.psum(partial_tile, 'rep')]
    reduce_sum x0 -> x1, other arithmetic: none -> 31.5 us  [shards(): gram_tile = jnp.sum(lax.all_gather(partial_tile, 'rep'), axis=0)]
where the time goes in v1:
time: 2270 us
  waiting for transfers between devices  1880 us (83%)
  blocking collectives  218 us (10%)
  local copies, waits for them, and re-layouts  59.2 us (3%)
  other arithmetic  52 us (2%)
  matrix products  48 us (2%)
    all_gather x1, waiting for transfers between devices, shards(): gram_tile = jnp.sum(lax.all_gather(partial_tile, 'rep'), axis=0)  1250 us
    reduce_scatter x1, waiting for transfers between devices, shards(): lax.psum_scatter(own_part.astype(jnp.bfloat16), 'rep', scatter_dimension=...  417 us
    all_gather x1, waiting for transfers between devices, shards(): lax.all_gather(cols_panel, 'row', axis=0, tiled=True)  146 us
    all_to_all x1, blocking collectives, shards(): lax.all_to_all(summed, 'col', split_axis=1, concat_axis=0, tiled=True)  141 us
    all_to_all x1, blocking collectives, shards(): lax.all_to_all(summed, 'row', split_axis=1, concat_axis=0, tiled=True)  77.3 us
    all_gather x1, waiting for transfers between devices, shards(): left_whole = lax.all_gather(rows_panel, 'col', axis=0, tiled=True)  64.5 us
    dot_general x1, matrix products, shards(): lax.dot_general(left_order, lax.all_gather(cols_panel, 'row', axis=0, til...  48 us
  transfers between devices with their start and end apart: 4, of which 4 were waited for; matrix products, arithmetic and copies ran while one was open for 1% of the time, Pallas kernels for 0%

profile of v1, /device:TPU:0, one launch (start us, length us, event | category | flops | bytes accessed | tf_op | source)
XLA Modules:
  0.0 2267.7 jit_solution(1987859502365859458)
XLA Ops:
  7.2 0.0 reduce-scatter.2.cloned.1.call-start
  7.2 30.8 %copy.5 = bf16[1,2048,6144]{1,2,0:T(8,128)(2,1)} copy(bf16[1,2048,6144]{2,1,0:T(8,128)(2,1)} %param.2) | data formatting | bytes 50331648 | tf_op args[0]
  38.0 0.0 reduce-scatter.2.cloned.1.call-update
  38.0 0.0 all-gather.5.cloned.1.call-start
  38.1 417.0 %reduce-scatter.2.cloned.1.call-done = bf16[512,6144]{0,1:T(8,128)(2,1)} async-done(((bf16[2048,6144]{0,1:T(8,128)(2,1)}), bf16[512,6144]{0,1:T(8,128)(2,1)}) %reduce-scatter.2.cloned.1.call-update) | async-done | bytes 6291472 | tf_op jit(solution)/shard_map/reduce_scatter | solution.py:9
  455.1 77.3 %all_to_all.38 = bf16[512,4,1536]{0,2,1:T(8,128)(2,1)} all-to-all(bf16[512,4,1536]{0,2,1:T(8,128)(2,1)} %bitcast.16), channel_id=1, replica_groups=mesh['rep'=4,'row'=4,'col'=2] {'row'}, dimensions={1} | all-to-all | bytes 12582912 | tf_op jit(solution)/shard_map/all_to_all | solution.py:10
  532.4 8.6 copy.6
  541.0 0.0 all-gather.5.cloned.1.call-update
  541.1 0.0 all-gather.7.cloned.1.call-start
  541.1 140.7 %all_to_all.39 = bf16[512,2,3072]{0,2,1:T(8,128)(2,1)} all-to-all(bf16[512,2,3072]{0,2,1:T(8,128)(2,1)} %bitcast.17), channel_id=1, replica_groups=mesh['rep'=4,'row'=4,'col'=2] {'col'}, dimensions={1} | all-to-all | bytes 12582912 | tf_op jit(solution)/shard_map/all_to_all | solution.py:11
  681.9 8.7 copy.8
  690.5 0.0 all-gather.7.cloned.1.call-update
  690.5 0.0 all-gather.9.cloned.1.call-start
  690.6 64.5 %all-gather.5.cloned.1.call-done = bf16[4096,1536]{1,0:T(8,128)(2,1)} async-done(((bf16[2048,1536]{1,0:T(8,128)(2,1)}), bf16[4096,1536]{1,0:T(8,128)(2,1)}) %all-gather.5.cloned.1.call-update) | async-done | bytes 12582928 | tf_op jit(solution)/shard_map/all_gather | solution.py:15
  755.1 11.1 copy.7
  766.2 145.7 %all-gather.7.cloned.1.call-done = bf16[4096,3072]{1,0:T(8,128)(2,1)} async-done(((bf16[1024,3072]{1,0:T(8,128)(2,1)}), bf16[4096,3072]{1,0:T(8,128)(2,1)}) %all-gather.7.cloned.1.call-update) | async-done | bytes 25165840 | tf_op jit(solution)/shard_map/all_gather | solution.py:23
  911.9 48.0 %fusion = f32[1536,3072]{1,0:T(8,128)} fusion(bf16[4096,1536]{1,0:T(8,128)(2,1)} %bitcast.22, bf16[4096,3072]{1,0:T(8,128)(2,1)} %all-gather.7.cloned.1.call-done), kind=kOutput, calls=%fused_computation.1 | convolution fusion | flops 38654705664 | bytes 56623104 | tf_op jit(solution)/shard_map/dot_general | solution.py:21
  960.0 0.0 all-gather.9.cloned.1.call-update
  960.0 1249.2 %all-gather.9.cloned.1.call-done = f32[6144,3072]{1,0:T(8,128)} async-done(((f32[1536,3072]{1,0:T(8,128)}), f32[6144,3072]{1,0:T(8,128)}) %all-gather.9.cloned.1.call-update) | async-done | bytes 75497488 | tf_op jit(solution)/shard_map/all_gather | solution.py:27
  2209.2 31.5 %reduce_sum.9 = f32[1536,3072]{1,0:T(8,128)} reduce(f32[4,1536,3072]{2,1,0:T(8,128)} %bitcast.10, f32[]{:T(128)} %constant.0.clone.1), dimensions={0}, to_apply=%region_1.0 | reduce | flops 14155776 | bytes 94371840 | tf_op jit(solution)/shard_map/reduce_sum | solution.py:27
  2240.7 20.5 multiply_add_fusion
Async XLA Ops:
  7.2 447.9 %reduce-scatter.2.cloned.1.call-start = ((), (), s32[]{:S(2)}) async-start(), calls=%async_computation.3 | async-start | bytes 31457280 | tf_op jit(solution)/shard_map/reduce_scatter | solution.py:9
  38.0 717.1 %all-gather.5.cloned.1.call-start = ((), (), s32[]{:S(2)}) async-start(), calls=%async_computation.4 | async-start | bytes 18874368 | tf_op jit(solution)/shard_map/all_gather | solution.py:15
  541.1 370.9 %all-gather.7.cloned.1.call-start = ((), (), s32[]{:S(2)}) async-start(), calls=%async_computation.5 | async-start | bytes 31457280 | tf_op jit(solution)/shard_map/all_gather | solution.py:23
  690.5 1518.6 %all-gather.9.cloned.1.call-start = ((), (), s32[]{:S(2)}) async-start(), calls=%async_computation.6 | async-start | bytes 94371840 | tf_op jit(solution)/shard_map/all_gather | solution.py:27
Sparse Core Ops, SparseCore 0:
  38.1 416.9 reduce-scatter.1
  541.2 213.8 all-gather.4
  756.7 155.2 all-gather.6
  960.1 1248.9 all-gather.8
